TPU v7x, 256 devices: a whole 4x4x8 slice. The times are simulated.
256 devices in a mesh: blk: 64 (over y_hi, x, z), grp: 4 (over y_lo, core).
Axes of the slice: x: 4, y: 4 (y_hi: 2, y_lo: 2; y = y_hi * 2 + y_lo), z: 8, core: 2. Of those that a mesh axis runs over, the one named last changes fastest.
Arguments:
- queries: float32 [32768, 256], P(('blk', 'grp')), may hold values from -20 to 20
- queue: float32 [131072, 256], P(('blk', 'grp')), may hold values from -16 to 16
- new_keys: float32 [32768, 256], P(('blk', 'grp')), may hold values from -3.6 to 3.6
- pos_index: int32 [32768], P(('blk', 'grp')), may hold values from 0 to 32767, as said below
- pointer: int32 [1], replicated, may hold values from 0 to 3
Outputs:
- losses: float32 [32768], P(('blk', 'grp'))
- queue_next: float32 [131072, 256], P(('blk', 'grp'))
Inputs may be any that keep to these rules, and one draw needn't show every extreme that they name: pos_index of a query lies in the same aligned block of 128 rows as the query itself, and within each block every row is named exactly once.
All inputs are finite; a program needn't handle non-finite values.
Results may differ from a plain program's by a relative error of at most 0.0012.
Values may be sent and summed in bfloat16 or wider, within the bound.
No kernel may reach another device: no remote copies, remote signals or barrier semaphores. Data moves between devices by JAX's collectives and lax.ppermute only.
A program may use at most 64 MiB of HBM per device.

v0:
```python
import jax
import jax.numpy as jnp
from jax import lax
from jax.sharding import Mesh
from jax.sharding import PartitionSpec as P

BLK = ("blk_0", "blk_1", "blk_2")
BLK_GRP = ("blk_0", "blk_1", "blk_2", "grp")
logit_scale = 5.0
epsilon = 1e-06


def in_order(pieces, dim):
    dims = list(pieces.shape[1:])
    dims[dim] *= pieces.shape[0]
    return jnp.moveaxis(pieces, 0, dim).reshape(dims)


def gather_in_order(x, axes, sequence):
    pieces = x[None]
    for k in sequence:
        pieces = lax.all_gather(pieces, axes[k], axis=0, tiled=True)
    block = [lax.axis_size(axes[k]) for k in reversed(sequence)]
    pieces = pieces.reshape(*block, *x.shape)
    turned = sorted(range(len(sequence)), key=lambda place: sequence[len(sequence) - 1 - place])
    return pieces.transpose(*turned, *range(len(sequence), pieces.ndim)).reshape(-1, *x.shape)


def gather_axes(x, axes, sequence, dim):
    return in_order(gather_in_order(x, axes, sequence), dim)


def from_everyone(x, axis):
    count = lax.axis_size(axis)
    return lax.all_to_all(jnp.broadcast_to(x[None], (count, *x.shape)), axis, 0, 0, tiled=True)


def gather_directly(x, axis, dim):
    pieces = from_everyone(x, axis)
    return in_order(pieces, dim)


def collected_together(x, axis):
    leaves = jax.tree.leaves(x)
    sequence = sorted(range(len(leaves)), key=lambda k: -leaves[k].size)
    width = (1, *leaves[sequence[0]].shape)[-1]
    lines = [
        jnp.pad(leaves[k].reshape(-1), (0, -leaves[k].size % width)).reshape(-1, width)
        for k in sequence
    ]
    both, at, found = (lax.all_gather(jnp.concatenate(lines), axis), 0, {})
    for k, line in zip(sequence, lines):
        share = both[:, at : at + len(line)].reshape(len(both), -1)
        found[k] = share[:, : leaves[k].size].reshape(-1, *leaves[k].shape)
        at += len(line)
    numbers = iter(range(len(leaves)))
    return jax.tree.map(lambda _: found[next(numbers)], x)


def combined_by_axis(x, axes, combine):
    for axis in axes:
        pieces = collected_together(x, axis)
        x = jax.tree.map(lambda part: part[0], pieces)
        for k in range(1, lax.axis_size(axis)):
            x = combine(x, jax.tree.map(lambda part: part[k], pieces))
    return x


def from_behind(value, axis, steps):
    count = lax.axis_size(axis)
    pairs = [(source, (source + steps) % count) for source in range(count)]
    return lax.ppermute(value, axis, pairs)


def normalize(rows):
    return rows / jnp.sqrt(jnp.sum(rows * rows, axis=1, keepdims=True) + epsilon)


def block_size(count, limit):
    size_now = max(1, min(count, limit))
    while count % size_now != 0:
        size_now = size_now - 1
    return size_now


def make_fold(query_rows, carry, piece):
    count = piece.shape[0]
    step_rows = block_size(count, max(8, 2**21 // query_rows.shape[0]))
    blocks = piece.reshape(count // step_rows, step_rows, piece.shape[1])

    def one_block(state, key_block):
        top, total = state
        scores = logit_scale * lax.dot_general(
            query_rows, key_block, (((1,), (1,)), ((), ())), preferred_element_type=jnp.float32
        )
        new_top = jnp.maximum(top, jnp.max(scores, axis=1))
        total = total * jnp.exp(top - new_top) + jnp.sum(jnp.exp(scores - new_top[:, None]), axis=1)
        return ((new_top, total), None)

    result, unused = lax.scan(one_block, carry, blocks)
    return result


def combine(first, second):
    new_top = jnp.maximum(first[0], second[0])
    total = first[1] * jnp.exp(first[0] - new_top) + second[1] * jnp.exp(second[0] - new_top)
    return (new_top, total)


def finish(query_rows, top, total, positive_rows):
    pos = logit_scale * jnp.sum(
        query_rows.astype(jnp.float32) * positive_rows.astype(jnp.float32), axis=1
    )
    high = jnp.maximum(top, pos)
    return high + jnp.log(jnp.exp(pos - high) + total * jnp.exp(top - high)) - pos


def per_device(queries, queue, new_keys, pos_index, pointer):
    qhat = normalize(queries).astype(jnp.bfloat16)
    keys = queue.astype(jnp.bfloat16)
    count = qhat.shape[0]
    device_rank = lax.axis_index(BLK) * lax.axis_size("grp") + lax.axis_index("grp")
    base = device_rank * count
    positives = jnp.take(new_keys.astype(jnp.bfloat16), pos_index - base, axis=0)
    group = gather_axes(qhat, BLK, (0, 1, 2), 0)
    rows_all = group.shape[0]
    start_state = (jnp.full((rows_all,), -1e30, jnp.float32), jnp.zeros((rows_all,), jnp.float32))
    partial_value = make_fold(group, start_state, gather_directly(keys, "grp", 0))
    top_all, total_all = combined_by_axis(partial_value, BLK, combine)
    offset = lax.axis_index(BLK) * count
    top = lax.dynamic_slice_in_dim(top_all, offset, count, 0)
    total = lax.dynamic_slice_in_dim(total_all, offset, count, 0)
    losses = finish(qhat, top, total, positives)
    incoming = from_behind(new_keys, BLK_GRP, 1)
    start = pointer[0] * new_keys.shape[0]
    queue_next = lax.dynamic_update_slice(queue, incoming, (start, jnp.int32(0)))
    return (losses, queue_next)


def solution(mesh):
    finer = Mesh(
        mesh.devices.reshape(2, 4, 8, mesh.shape["grp"]), ("blk_0", "blk_1", "blk_2", "grp")
    )
    return jax.shard_map(
        per_device,
        mesh=finer,
        in_specs=(P(BLK_GRP, None), P(BLK_GRP, None), P(BLK_GRP, None), P(BLK_GRP), P()),
        out_specs=(P(BLK_GRP), P(BLK_GRP, None)),
        check_vma=False,
    )
```

profile of v0, /device:TPU:8, one launch (start us, length us, event | category | flops | bytes accessed | tf_op | source)
XLA Modules:
  0.0 186.8 jit_solution(409798083042916813)
XLA Ops:
  7.2 0.0 all-gather.9.cloned.1.call-start
  7.2 1.0 copy.21
  8.3 1.0 multiply_reduce_fusion.1
  9.3 0.7 compare_and_fusion
  10.0 0.9 convert_element_type.18
  10.9 0.8 gather_fusion
  11.7 1.1 multiply_reduce_fusion
  12.8 6.4 %all-gather = bf16[256,256]{1,0:T(8,128)(2,1)S(1)} all-gather(bf16[128,256]{1,0:T(8,128)(2,1)S(1)} %get-tuple-element.61), channel_id=2, replica_groups=mesh['blk_0'=2,'blk_1'=4,'blk_2'=8,'grp'=4] {'blk_0'}, dimensions={0}, use_global_device_ids=true | all-gather | bytes 196608 | tf_op jit(solution)/shard_map/all_gather | solution.py:22
  19.3 14.2 %all_gather.28 = bf16[8,128,256]{2,1,0:T(8,128)(2,1)} all-gather(bf16[2,128,256]{2,1,0:T(8,128)(2,1)S(1)} %bitcast.144), channel_id=1, replica_groups=mesh['blk_0'=2,'blk_1'=4,'blk_2'=8,'grp'=4] {'blk_1'}, dimensions={0}, use_global_device_ids=true | all-gather | bytes 655360 | tf_op jit(solution)/shard_map/all_gather | solution.py:22
  33.4 0.0 all-gather.9.cloned.1.call-update
  33.5 1.1 broadcast_in_dim.31
  34.6 5.6 %all-to-all-start = ((bf16[4,512,256]{2,1,0:T(8,128)(2,1)}), bf16[4,512,256]{2,1,0:T(8,128)(2,1)S(1)}, u32[]{:S(2)}, u32[]{:S(2)}) async-start(bf16[4,512,256]{2,1,0:T(8,128)(2,1)} %broadcast_in_dim.31), calls=%async_computation | async-start | bytes 2097152 | tf_op jit(solution)/shard_map/all_to_all | solution.py:35
  40.2 0.1 collective-permute-start
  41.0 13.4 %collective-permute-done = f32[128,256]{1,0:T(8,128)S(1)} collective-permute-done((f32[128,256]{1,0:T(8,128)}, f32[128,256]{1,0:T(8,128)S(1)}, u32[]{:S(2)}, u32[]{:S(2)}) %collective-permute-start) | collective-permute-done | bytes 131104 | tf_op jit(solution)/shard_map/ppermute | solution.py:72
  54.4 0.0 copy-start
  54.4 36.3 %all-gather.9.cloned.1.call-done = bf16[64,128,256]{2,1,0:T(8,128)(2,1)} async-done(((bf16[8,128,256]{2,1,0:T(8,128)(2,1)}), bf16[64,128,256]{2,1,0:T(8,128)(2,1)}) %all-gather.9.cloned.1.call-update) | async-done | bytes 4194320 | tf_op jit(solution)/shard_map/all_gather | solution.py:22
  90.7 4.6 %copy.8 = bf16[2,4,8,128,256]{4,3,2,1,0:T(8,128)(2,1)} copy(bf16[2,4,8,128,256]{4,3,0,1,2:T(8,128)(2,1)} %bitcast.140) | data formatting | bytes 8388608 | tf_op jit(solution)/shard_map/transpose | solution.py:26
  95.3 0.0 all-to-all-done
  95.3 0.0 copy-done
  95.3 38.3 %while.13 = (s32[]{:T(128)}, f32[8192]{0:T(1024)S(1)}, f32[8192]{0:T(1024)S(1)}, bf16[8,256,256]{2,1,0:T(8,128)(2,1)S(1)}, bf16[8192,256]{1,0:T(8,128)(2,1)}, /*index=5*/s32[]{:T(128)}, s32[]{:T(128)}) while((s32[]{:T(128)}, f32[8192]{0:T(1024)S(1)}, f32[8192]{0:T(1024)S(1)}, bf16[8,256,256]{2,1,0:T(8,128)(2,1)S(1)}, ...), condition=%wide.region_4.5_spmd.clone, body=%wide.region_1.4_spmd.clone.sunk | while | flops 1082171392 | bytes 21528676 | solution.py:100
  95.3 3.5 %fusion.40 = (f32[8192]{0:T(1024)S(1)}, f32[256,8192]{1,0:T(8,128)S(1)}) fusion(bf16[8192,256]{1,0:T(8,128)(2,1)} %get-tuple-element.149, bf16[8,256,256]{2,1,0:T(8,128)(2,1)S(1)} %get-tuple-element.148, s32[]{:T(128)S(6)} %copy.12), kind=kOutput, calls=%fused_computation.71.clone.1 | convolution fusion | flops 1077927936 | bytes 12746756 | tf_op jit(solution)/shard_map/while/body/eval_jaxpr/dot_general | solution.py:93
  98.9 1.2 exponential_reduce_fusion.2
  100.1 3.5 %fusion.40 = (f32[8192]{0:T(1024)S(1)}, f32[256,8192]{1,0:T(8,128)S(1)}) fusion(bf16[8192,256]{1,0:T(8,128)(2,1)} %get-tuple-element.149, bf16[8,256,256]{2,1,0:T(8,128)(2,1)S(1)} %get-tuple-element.148, s32[]{:T(128)S(6)} %copy.12), kind=kOutput, calls=%fused_computation.71.clone.1 | convolution fusion | flops 1077927936 | bytes 12746756 | tf_op jit(solution)/shard_map/while/body/eval_jaxpr/dot_general | solution.py:93
  103.6 1.2 exponential_reduce_fusion.2
  104.9 3.5 %fusion.40 = (f32[8192]{0:T(1024)S(1)}, f32[256,8192]{1,0:T(8,128)S(1)}) fusion(bf16[8192,256]{1,0:T(8,128)(2,1)} %get-tuple-element.149, bf16[8,256,256]{2,1,0:T(8,128)(2,1)S(1)} %get-tuple-element.148, s32[]{:T(128)S(6)} %copy.12), kind=kOutput, calls=%fused_computation.71.clone.1 | convolution fusion | flops 1077927936 | bytes 12746756 | tf_op jit(solution)/shard_map/while/body/eval_jaxpr/dot_general | solution.py:93
  108.4 1.2 exponential_reduce_fusion.2
  109.7 3.5 %fusion.40 = (f32[8192]{0:T(1024)S(1)}, f32[256,8192]{1,0:T(8,128)S(1)}) fusion(bf16[8192,256]{1,0:T(8,128)(2,1)} %get-tuple-element.149, bf16[8,256,256]{2,1,0:T(8,128)(2,1)S(1)} %get-tuple-element.148, s32[]{:T(128)S(6)} %copy.12), kind=kOutput, calls=%fused_computation.71.clone.1 | convolution fusion | flops 1077927936 | bytes 12746756 | tf_op jit(solution)/shard_map/while/body/eval_jaxpr/dot_general | solution.py:93
  113.2 1.2 exponential_reduce_fusion.2
  114.5 3.5 %fusion.40 = (f32[8192]{0:T(1024)S(1)}, f32[256,8192]{1,0:T(8,128)S(1)}) fusion(bf16[8192,256]{1,0:T(8,128)(2,1)} %get-tuple-element.149, bf16[8,256,256]{2,1,0:T(8,128)(2,1)S(1)} %get-tuple-element.148, s32[]{:T(128)S(6)} %copy.12), kind=kOutput, calls=%fused_computation.71.clone.1 | convolution fusion | flops 1077927936 | bytes 12746756 | tf_op jit(solution)/shard_map/while/body/eval_jaxpr/dot_general | solution.py:93
  118.0 1.2 exponential_reduce_fusion.2
  119.3 3.5 %fusion.40 = (f32[8192]{0:T(1024)S(1)}, f32[256,8192]{1,0:T(8,128)S(1)}) fusion(bf16[8192,256]{1,0:T(8,128)(2,1)} %get-tuple-element.149, bf16[8,256,256]{2,1,0:T(8,128)(2,1)S(1)} %get-tuple-element.148, s32[]{:T(128)S(6)} %copy.12), kind=kOutput, calls=%fused_computation.71.clone.1 | convolution fusion | flops 1077927936 | bytes 12746756 | tf_op jit(solution)/shard_map/while/body/eval_jaxpr/dot_general | solution.py:93
  122.8 1.2 exponential_reduce_fusion.2
  124.1 3.5 %fusion.40 = (f32[8192]{0:T(1024)S(1)}, f32[256,8192]{1,0:T(8,128)S(1)}) fusion(bf16[8192,256]{1,0:T(8,128)(2,1)} %get-tuple-element.149, bf16[8,256,256]{2,1,0:T(8,128)(2,1)S(1)} %get-tuple-element.148, s32[]{:T(128)S(6)} %copy.12), kind=kOutput, calls=%fused_computation.71.clone.1 | convolution fusion | flops 1077927936 | bytes 12746756 | tf_op jit(solution)/shard_map/while/body/eval_jaxpr/dot_general | solution.py:93
  127.6 1.2 exponential_reduce_fusion.2
  128.9 3.5 %fusion.40 = (f32[8192]{0:T(1024)S(1)}, f32[256,8192]{1,0:T(8,128)S(1)}) fusion(bf16[8192,256]{1,0:T(8,128)(2,1)} %get-tuple-element.149, bf16[8,256,256]{2,1,0:T(8,128)(2,1)S(1)} %get-tuple-element.148, s32[]{:T(128)S(6)} %copy.12), kind=kOutput, calls=%fused_computation.71.clone.1 | convolution fusion | flops 1077927936 | bytes 12746756 | tf_op jit(solution)/shard_map/while/body/eval_jaxpr/dot_general | solution.py:93
  132.4 1.2 exponential_reduce_fusion.2
  133.6 0.1 maximum_bitcast_fusion
  133.7 6.4 %all-gather.4 = f32[2,2,8192]{2,1,0:T(2,128)S(1)} all-gather(f32[1,2,8192]{2,1,0:T(2,128)S(1)} %maximum_bitcast_fusion), channel_id=3, replica_groups=mesh['blk_0'=2,'blk_1'=4,'blk_2'=8,'grp'=4] {'blk_0'}, dimensions={0}, use_global_device_ids=true | all-gather | bytes 196608 | tf_op jit(solution)/shard_map/all_gather | solution.py:51
  140.1 0.1 fusion.14
  140.3 0.1 maximum_bitcast_fusion.1
  140.3 12.7 %all-gather.5 = f32[4,2,8192]{2,1,0:T(2,128)S(1)} all-gather(f32[1,2,8192]{2,1,0:T(2,128)S(1)} %maximum_bitcast_fusion.1), channel_id=4, replica_groups=mesh['blk_0'=2,'blk_1'=4,'blk_2'=8,'grp'=4] {'blk_1'}, dimensions={0}, use_global_device_ids=true | all-gather | bytes 327680 | tf_op jit(solution)/shard_map/all_gather | solution.py:51
  153.1 0.3 fusion.5
  153.4 0.1 maximum_bitcast_fusion.2
  153.5 25.3 %all-gather.6 = f32[8,2,8192]{2,1,0:T(2,128)S(1)} all-gather(f32[1,2,8192]{2,1,0:T(2,128)S(1)} %maximum_bitcast_fusion.2), channel_id=5, replica_groups=mesh['blk_0'=2,'blk_1'=4,'blk_2'=8,'grp'=4] {'blk_2'}, dimensions={0}, use_global_device_ids=true | all-gather | bytes 589824 | tf_op jit(solution)/shard_map/all_gather | solution.py:51
  178.7 0.5 fusion.34
  179.3 0.1 multiply_add_fusion
  179.3 0.6 add_subtract_fusion
  (31 shorter events, 0.3 us)
Async XLA Ops:
  7.2 83.6 %all-gather.9.cloned.1.call-start = ((), (), s32[]{:S(2)}) async-start(), calls=%async_computation.1 | async-start | bytes 4718592 | tf_op jit(solution)/shard_map/all_gather | solution.py:22
  34.6 60.8 %all-to-all-start = ((bf16[4,512,256]{2,1,0:T(8,128)(2,1)}), bf16[4,512,256]{2,1,0:T(8,128)(2,1)S(1)}, u32[]{:S(2)}, u32[]{:S(2)}) async-start(bf16[4,512,256]{2,1,0:T(8,128)(2,1)} %broadcast_in_dim.31), calls=%async_computation | async-start | bytes 2097152 | tf_op jit(solution)/shard_map/all_to_all | solution.py:35
  40.2 14.2 %collective-permute-start = (f32[128,256]{1,0:T(8,128)}, f32[128,256]{1,0:T(8,128)S(1)}, u32[]{:S(2)}, u32[]{:S(2)}) collective-permute-start(f32[128,256]{1,0:T(8,128)} %param.9), channel_id=1, source_target_pairs={{0,1},{1,2},{2,3},{3,4},{4,5},{5,6},{6,7},{7,8},{8,9},{9,10},{10,1... | collective-permute-start | bytes 393224 | tf_op jit(solution)/shard_map/ppermute | solution.py:72
  54.4 40.9 %copy-start = (f32[512,256]{1,0:T(8,128)}, f32[512,256]{1,0:T(8,128)S(1)}, u32[]{:S(2)}) copy-start(f32[512,256]{1,0:T(8,128)S(1)} %constant_dynamic-update-slice_fusion) | copy-start | bytes 1572868
Sparse Core Ops, SparseCore 0:
  33.6 57.1 all-gather.8
where the time goes:
time: 187 us
  blocking collectives  65 us (35%)
  waiting for transfers between devices  49.7 us (27%)
  matrix products  27.9 us (15%)
  other arithmetic  15 us (8%)
  between operations  14.8 us (8%)
  local copies, waits for them, and re-layouts  8.14 us (4%)
  starting transfers between devices  5.78 us (3%)
    all_gather x3, blocking collectives, collected_together(): both, at, found = (lax.all_gather(jnp.concatenate(lines), axis), 0, {})  44.4 us
    all_gather x1, waiting for transfers between devices, gather_in_order(): pieces = lax.all_gather(pieces, axes[k], axis=0, tiled=True)  36.3 us
    dot_general x8, matrix products, one_block(): lax.dot_general(query_rows, key_block, (((1,), (1,)), ((), ())), preferre...  27.9 us
    all_gather x2, blocking collectives, gather_in_order(): pieces = lax.all_gather(pieces, axes[k], axis=0, tiled=True)  20.6 us
    ppermute x1, waiting for transfers between devices, from_behind(): return lax.ppermute(value, axis, pairs)  13.4 us
    reduce_sum x8, other arithmetic, one_block(): jnp.sum(jnp.exp(scores - new_top[:, None]), axis=1)  9.67 us
    all_to_all x1, starting transfers between devices, from_everyone(): lax.all_to_all(jnp.broadcast_to(x[None], (count, *x.shape)), axis, 0, 0,...  5.62 us
    transpose x1, local copies, waits for them, and re-layouts, gather_in_order(): pieces.transpose(*turned, *range(len(sequence), pieces.ndim))  4.62 us
  transfers between devices with their start and end apart: 3, of which 2 were waited for; matrix products, arithmetic and copies ran while one was open for 3% of the time, Pallas kernels for 0%

commit v1 on v0

--- a/solution.py
+++ b/solution.py
@@ -19,7 +19,9 @@
 def gather_in_order(x, axes, sequence):
     pieces = x[None]
     for k in sequence:
-        pieces = lax.all_gather(pieces, axes[k], axis=0, tiled=True)
+        pieces = jnp.concatenate(
+            lax.all_to_all(jnp.stack([pieces] * lax.axis_size(axes[k])), axes[k], 0, 0), axis=0
+        )
     block = [lax.axis_size(axes[k]) for k in reversed(sequence)]
     pieces = pieces.reshape(*block, *x.shape)
     turned = sorted(range(len(sequence)), key=lambda place: sequence[len(sequence) - 1 - place])

time: 187 us -> 242 us (1.29)
  waiting for transfers between devices: 49.7 us -> 107 us
  between operations: 14.8 us -> 1.41 us
  starting transfers between devices: 5.78 us -> 13.4 us
  local copies, waits for them, and re-layouts: 8.14 us -> 10.8 us
    all_to_all x0 -> x1, waiting for transfers between devices: none -> 93.5 us  [gather_in_order(): lax.all_to_all(jnp.stack([pieces] * lax.axis_size(axes[k])), axes[k], 0, 0)]
    all_gather x1 -> x0, waiting for transfers between devices: 36.3 us -> none  [gather_in_order(): pieces = lax.all_gather(pieces, axes[k], axis=0, tiled=True)]
    all_to_all x0 -> x2, blocking collectives: none -> 21.5 us  [gather_in_order(): lax.all_to_all(jnp.stack([pieces] * lax.axis_size(axes[k])), axes[k], 0, 0)]
    all_gather x2 -> x0, blocking collectives: 20.6 us -> none  [gather_in_order(): pieces = lax.all_gather(pieces, axes[k], axis=0, tiled=True)]
    all_to_all x0 -> x1, starting transfers between devices: none -> 8.47 us  [gather_in_order(): lax.all_to_all(jnp.stack([pieces] * lax.axis_size(axes[k])), axes[k], 0, 0)]
    another operation x0 -> x2, local copies, waits for them, and re-layouts: none -> 2.5 us  [gather_in_order(): jnp.stack([pieces] * lax.axis_size(axes[k]))]
  transfers between devices with their start and end apart: 3 -> 3, of which waited for: 2 -> 2; matrix products, arithmetic and copies ran while one was open for 3% -> 2% of each run, Pallas kernels for 0% -> 0%
where the time goes in v1:
time: 242 us
  waiting for transfers between devices  107 us (44%)
  blocking collectives  65.7 us (27%)
  matrix products  27.9 us (12%)
  other arithmetic  15 us (6%)
  starting transfers between devices  13.4 us (6%)
  local copies, waits for them, and re-layouts  10.8 us (4%)
    all_to_all x1, waiting for transfers between devices, gather_in_order(): lax.all_to_all(jnp.stack([pieces] * lax.axis_size(axes[k])), axes[k], 0, 0)  93.5 us
    all_gather x3, blocking collectives, collected_together(): both, at, found = (lax.all_gather(jnp.concatenate(lines), axis), 0, {})  44.2 us
    dot_general x8, matrix products, one_block(): lax.dot_general(query_rows, key_block, (((1,), (1,)), ((), ())), preferre...  27.9 us
    all_to_all x2, blocking collectives, gather_in_order(): lax.all_to_all(jnp.stack([pieces] * lax.axis_size(axes[k])), axes[k], 0, 0)  21.5 us
    ppermute x1, waiting for transfers between devices, from_behind(): return lax.ppermute(value, axis, pairs)  13.4 us
    reduce_sum x8, other arithmetic, one_block(): jnp.sum(jnp.exp(scores - new_top[:, None]), axis=1)  9.67 us
    all_to_all x1, starting transfers between devices, gather_in_order(): lax.all_to_all(jnp.stack([pieces] * lax.axis_size(axes[k])), axes[k], 0, 0)  8.47 us
  transfers between devices with their start and end apart: 3, of which 2 were waited for; matrix products, arithmetic and copies ran while one was open for 2% of the time, Pallas kernels for 0%

profile of v1, /device:TPU:8, one launch (start us, length us, event | category | flops | bytes accessed | tf_op | source)
XLA Modules:
  0.0 241.6 jit_solution(14987305493462223286)
XLA Ops:
  0.6 1.0 copy.21
  1.7 1.0 multiply_reduce_fusion.1
  2.7 0.7 compare_and_fusion
  3.4 0.9 convert_element_type.18
  4.3 0.8 gather_fusion
  5.2 1.1 multiply_reduce_fusion
  6.3 9.3 %all_to_all.20 = bf16[2,1,128,256]{3,2,1,0:T(8,128)(2,1)S(1)} all-to-all(bf16[2,1,128,256]{3,2,1,0:T(8,128)(2,1)S(1)} %pad_maximum_fusion), channel_id=1, replica_groups=mesh['blk_0'=2,'blk_1'=4,'blk_2'=8,'grp'=4] {'blk_0'}, dimensions={0} | all-to-all | bytes 262144 | tf_op jit(solution)/shard_map/all_to_all | solution.py:23
  15.6 12.2 %all_to_all.21 = bf16[4,2,128,256]{3,2,1,0:T(8,128)(2,1)S(1)} all-to-all(bf16[4,2,128,256]{3,2,1,0:T(8,128)(2,1)S(1)} %stack.10), channel_id=1, replica_groups=mesh['blk_0'=2,'blk_1'=4,'blk_2'=8,'grp'=4] {'blk_1'}, dimensions={0} | all-to-all | bytes 1048576 | tf_op jit(solution)/shard_map/all_to_all | solution.py:23
  27.8 0.0 copy-start.1
  27.8 2.5 %stack.11 = bf16[8,8,128,256]{3,2,1,0:T(8,128)(2,1)} broadcast(bf16[8,128,256]{2,1,0:T(8,128)(2,1)S(1)} %bitcast.144), dimensions={1,2,3} | broadcast | bytes 4718592 | tf_op jit(solution)/shard_map/stack | solution.py:23
  30.3 8.5 %all-to-all-start.3 = ((bf16[8,8,128,256]{3,2,1,0:T(8,128)(2,1)}), bf16[8,8,128,256]{3,2,1,0:T(8,128)(2,1)}, u32[]{:S(2)}, u32[]{:S(2)}) async-start(bf16[8,8,128,256]{3,2,1,0:T(8,128)(2,1)} %stack.11), calls=%async_computation.3 | async-start | bytes 8388608 | tf_op jit(solution)/shard_map/all_to_all | solution.py:23
  38.8 93.5 %all-to-all-done.3 = bf16[8,8,128,256]{3,2,1,0:T(8,128)(2,1)} async-done(((bf16[8,8,128,256]{3,2,1,0:T(8,128)(2,1)}), bf16[8,8,128,256]{3,2,1,0:T(8,128)(2,1)}, u32[]{:S(2)}, u32[]{:S(2)}) %all-to-all-start.3) | async-done | bytes 4194336 | tf_op jit(solution)/shard_map/all_to_all | solution.py:23
  132.3 1.1 broadcast_in_dim.28
  133.4 4.8 %all-to-all-start = ((bf16[4,512,256]{2,1,0:T(8,128)(2,1)}), bf16[4,512,256]{2,1,0:T(8,128)(2,1)S(1)}, u32[]{:S(2)}, u32[]{:S(2)}) async-start(bf16[4,512,256]{2,1,0:T(8,128)(2,1)} %broadcast_in_dim.28), calls=%async_computation | async-start | bytes 2097152 | tf_op jit(solution)/shard_map/all_to_all | solution.py:37
  138.2 0.0 copy-done.1
  138.2 0.1 collective-permute-start
  139.0 13.4 %collective-permute-done = f32[128,256]{1,0:T(8,128)S(1)} collective-permute-done((f32[128,256]{1,0:T(8,128)S(1)}, f32[128,256]{1,0:T(8,128)S(1)}, u32[]{:S(2)}, u32[]{:S(2)}) %collective-permute-start) | collective-permute-done | bytes 131104 | tf_op jit(solution)/shard_map/ppermute | solution.py:74
  152.4 0.0 copy-start
  152.4 4.8 %copy.8 = bf16[2,4,8,128,256]{4,3,2,1,0:T(8,128)(2,1)} copy(bf16[2,4,8,128,256]{4,3,0,1,2:T(8,128)(2,1)} %bitcast.5) | data formatting | bytes 8388608 | tf_op jit(solution)/shard_map/transpose | solution.py:28
  157.2 0.0 all-to-all-done
  157.2 0.0 copy-done
  157.2 38.3 %while.13 = (s32[]{:T(128)}, f32[8192]{0:T(1024)S(1)}, f32[8192]{0:T(1024)S(1)}, bf16[8,256,256]{2,1,0:T(8,128)(2,1)S(1)}, bf16[8192,256]{1,0:T(8,128)(2,1)}, /*index=5*/s32[]{:T(128)}, s32[]{:T(128)}) while((s32[]{:T(128)}, f32[8192]{0:T(1024)S(1)}, f32[8192]{0:T(1024)S(1)}, bf16[8,256,256]{2,1,0:T(8,128)(2,1)S(1)}, ...), condition=%wide.region_4.5_spmd.clone, body=%wide.region_1.4_spmd.clone.sunk | while | flops 1082171392 | bytes 21528676 | solution.py:102
  157.2 3.5 %fusion.40 = (f32[8192]{0:T(1024)S(1)}, f32[256,8192]{1,0:T(8,128)S(1)}) fusion(bf16[8192,256]{1,0:T(8,128)(2,1)} %get-tuple-element.149, bf16[8,256,256]{2,1,0:T(8,128)(2,1)S(1)} %get-tuple-element.148, s32[]{:T(128)S(6)} %copy.12), kind=kOutput, calls=%fused_computation.72.clone.1 | convolution fusion | flops 1077927936 | bytes 12746756 | tf_op jit(solution)/shard_map/while/body/eval_jaxpr/dot_general | solution.py:95
  160.8 1.2 exponential_reduce_fusion.2
  162.0 3.5 %fusion.40 = (f32[8192]{0:T(1024)S(1)}, f32[256,8192]{1,0:T(8,128)S(1)}) fusion(bf16[8192,256]{1,0:T(8,128)(2,1)} %get-tuple-element.149, bf16[8,256,256]{2,1,0:T(8,128)(2,1)S(1)} %get-tuple-element.148, s32[]{:T(128)S(6)} %copy.12), kind=kOutput, calls=%fused_computation.72.clone.1 | convolution fusion | flops 1077927936 | bytes 12746756 | tf_op jit(solution)/shard_map/while/body/eval_jaxpr/dot_general | solution.py:95
  165.6 1.2 exponential_reduce_fusion.2
  166.8 3.5 %fusion.40 = (f32[8192]{0:T(1024)S(1)}, f32[256,8192]{1,0:T(8,128)S(1)}) fusion(bf16[8192,256]{1,0:T(8,128)(2,1)} %get-tuple-element.149, bf16[8,256,256]{2,1,0:T(8,128)(2,1)S(1)} %get-tuple-element.148, s32[]{:T(128)S(6)} %copy.12), kind=kOutput, calls=%fused_computation.72.clone.1 | convolution fusion | flops 1077927936 | bytes 12746756 | tf_op jit(solution)/shard_map/while/body/eval_jaxpr/dot_general | solution.py:95
  170.3 1.2 exponential_reduce_fusion.2
  171.6 3.5 %fusion.40 = (f32[8192]{0:T(1024)S(1)}, f32[256,8192]{1,0:T(8,128)S(1)}) fusion(bf16[8192,256]{1,0:T(8,128)(2,1)} %get-tuple-element.149, bf16[8,256,256]{2,1,0:T(8,128)(2,1)S(1)} %get-tuple-element.148, s32[]{:T(128)S(6)} %copy.12), kind=kOutput, calls=%fused_computation.72.clone.1 | convolution fusion | flops 1077927936 | bytes 12746756 | tf_op jit(solution)/shard_map/while/body/eval_jaxpr/dot_general | solution.py:95
  175.1 1.2 exponential_reduce_fusion.2
  176.4 3.5 %fusion.40 = (f32[8192]{0:T(1024)S(1)}, f32[256,8192]{1,0:T(8,128)S(1)}) fusion(bf16[8192,256]{1,0:T(8,128)(2,1)} %get-tuple-element.149, bf16[8,256,256]{2,1,0:T(8,128)(2,1)S(1)} %get-tuple-element.148, s32[]{:T(128)S(6)} %copy.12), kind=kOutput, calls=%fused_computation.72.clone.1 | convolution fusion | flops 1077927936 | bytes 12746756 | tf_op jit(solution)/shard_map/while/body/eval_jaxpr/dot_general | solution.py:95
  179.9 1.2 exponential_reduce_fusion.2
  181.2 3.5 %fusion.40 = (f32[8192]{0:T(1024)S(1)}, f32[256,8192]{1,0:T(8,128)S(1)}) fusion(bf16[8192,256]{1,0:T(8,128)(2,1)} %get-tuple-element.149, bf16[8,256,256]{2,1,0:T(8,128)(2,1)S(1)} %get-tuple-element.148, s32[]{:T(128)S(6)} %copy.12), kind=kOutput, calls=%fused_computation.72.clone.1 | convolution fusion | flops 1077927936 | bytes 12746756 | tf_op jit(solution)/shard_map/while/body/eval_jaxpr/dot_general | solution.py:95
  184.7 1.2 exponential_reduce_fusion.2
  186.0 3.5 %fusion.40 = (f32[8192]{0:T(1024)S(1)}, f32[256,8192]{1,0:T(8,128)S(1)}) fusion(bf16[8192,256]{1,0:T(8,128)(2,1)} %get-tuple-element.149, bf16[8,256,256]{2,1,0:T(8,128)(2,1)S(1)} %get-tuple-element.148, s32[]{:T(128)S(6)} %copy.12), kind=kOutput, calls=%fused_computation.72.clone.1 | convolution fusion | flops 1077927936 | bytes 12746756 | tf_op jit(solution)/shard_map/while/body/eval_jaxpr/dot_general | solution.py:95
  189.5 1.2 exponential_reduce_fusion.2
  190.8 3.5 %fusion.40 = (f32[8192]{0:T(1024)S(1)}, f32[256,8192]{1,0:T(8,128)S(1)}) fusion(bf16[8192,256]{1,0:T(8,128)(2,1)} %get-tuple-element.149, bf16[8,256,256]{2,1,0:T(8,128)(2,1)S(1)} %get-tuple-element.148, s32[]{:T(128)S(6)} %copy.12), kind=kOutput, calls=%fused_computation.72.clone.1 | convolution fusion | flops 1077927936 | bytes 12746756 | tf_op jit(solution)/shard_map/while/body/eval_jaxpr/dot_general | solution.py:95
  194.3 1.2 exponential_reduce_fusion.2
  195.5 0.1 maximum_bitcast_fusion
  195.6 6.4 %all-gather.3 = f32[2,2,8192]{2,1,0:T(2,128)S(1)} all-gather(f32[1,2,8192]{2,1,0:T(2,128)S(1)} %maximum_bitcast_fusion), channel_id=2, replica_groups=mesh['blk_0'=2,'blk_1'=4,'blk_2'=8,'grp'=4] {'blk_0'}, dimensions={0}, use_global_device_ids=true | all-gather | bytes 196608 | tf_op jit(solution)/shard_map/all_gather | solution.py:53
  202.0 0.1 fusion.14
  202.2 0.1 maximum_bitcast_fusion.1
  202.2 12.3 %all-gather.4 = f32[4,2,8192]{2,1,0:T(2,128)S(1)} all-gather(f32[1,2,8192]{2,1,0:T(2,128)S(1)} %maximum_bitcast_fusion.1), channel_id=3, replica_groups=mesh['blk_0'=2,'blk_1'=4,'blk_2'=8,'grp'=4] {'blk_1'}, dimensions={0}, use_global_device_ids=true | all-gather | bytes 327680 | tf_op jit(solution)/shard_map/all_gather | solution.py:53
  214.5 0.3 fusion.5
  214.8 0.1 maximum_bitcast_fusion.2
  214.9 25.5 %all-gather.5 = f32[8,2,8192]{2,1,0:T(2,128)S(1)} all-gather(f32[1,2,8192]{2,1,0:T(2,128)S(1)} %maximum_bitcast_fusion.2), channel_id=4, replica_groups=mesh['blk_0'=2,'blk_1'=4,'blk_2'=8,'grp'=4] {'blk_2'}, dimensions={0}, use_global_device_ids=true | all-gather | bytes 589824 | tf_op jit(solution)/shard_map/all_gather | solution.py:53
  240.4 0.5 fusion.34
  240.9 0.1 multiply_add_fusion
  241.0 0.6 add_subtract_fusion
  (33 shorter events, 0.4 us)
Async XLA Ops:
  27.8 110.4 %copy-start.1 = (f32[128,256]{1,0:T(8,128)S(1)}, f32[128,256]{1,0:T(8,128)}, u32[]{:S(2)}) copy-start(f32[128,256]{1,0:T(8,128)} %param.9) | copy-start | bytes 393220
  30.3 102.0 %all-to-all-start.3 = ((bf16[8,8,128,256]{3,2,1,0:T(8,128)(2,1)}), bf16[8,8,128,256]{3,2,1,0:T(8,128)(2,1)}, u32[]{:S(2)}, u32[]{:S(2)}) async-start(bf16[8,8,128,256]{3,2,1,0:T(8,128)(2,1)} %stack.11), calls=%async_computation.3 | async-start | bytes 8388608 | tf_op jit(solution)/shard_map/all_to_all | solution.py:23
  133.4 23.9 %all-to-all-start = ((bf16[4,512,256]{2,1,0:T(8,128)(2,1)}), bf16[4,512,256]{2,1,0:T(8,128)(2,1)S(1)}, u32[]{:S(2)}, u32[]{:S(2)}) async-start(bf16[4,512,256]{2,1,0:T(8,128)(2,1)} %broadcast_in_dim.28), calls=%async_computation | async-start | bytes 2097152 | tf_op jit(solution)/shard_map/all_to_all | solution.py:37
  138.2 14.2 %collective-permute-start = (f32[128,256]{1,0:T(8,128)S(1)}, f32[128,256]{1,0:T(8,128)S(1)}, u32[]{:S(2)}, u32[]{:S(2)}) collective-permute-start(f32[128,256]{1,0:T(8,128)S(1)} %copy-done.1), channel_id=1, source_target_pairs={{0,1},{1,2},{2,3},{3,4},{4,5},{5,6},{6,7},{7,8},{8,9},{9,10},{10,1... | collective-permute-start | bytes 393224 | tf_op jit(solution)/shard_map/ppermute | solution.py:74
  152.4 4.8 %copy-start = (f32[512,256]{1,0:T(8,128)}, f32[512,256]{1,0:T(8,128)S(1)}, u32[]{:S(2)}) copy-start(f32[512,256]{1,0:T(8,128)S(1)} %constant_dynamic-update-slice_fusion) | copy-start | bytes 1572868
